TPU v7x, 32 devices: a whole 2x2x4 slice. The times are simulated.
32 devices in a mesh: node: 8 (over z, core), expert: 4 (over y, x).
Axes of the slice: x: 2, y: 2, z: 4, core: 2. Of those that a mesh axis runs over, the one named last changes fastest.
Arguments:
- numerators: bfloat16 [8, 4, 1536, 1536], P('node', 'expert'), may hold values from -6 to 6
- push_weights: float32 [8], replicated, may hold values from 0.5 to 2
- tokens: bfloat16 [8, 512, 1536], P('node', 'expert'), may hold values from -6 to 6
- cotangent: bfloat16 [8, 512, 1536], P('node', 'expert'), may hold values from -6 to 6
- routing: int32 [8, 512, 2], P('node', 'expert'), may hold values from 0 to 3, all different within a row; in each aligned block of 128 rows (0 to 127, 128 to 255, ..., all dimensions but the last counted through in order) at most 81 rows name the same one
- gates: float32 [8, 512, 2], P('node', 'expert'), may hold values from 0.1 to 1
Outputs:
- averaged: float32 [4, 1536, 1536], P('expert', 'node')
Inputs may be any that keep to these rules, and one draw needn't show every extreme that they name: `routing`: each row names 2 different experts; in each aligned block of 128 rows (the rows of one device) no expert is named by more than 81 rows, and in some block some expert is named by exactly 81 rows.
All inputs are finite; a program needn't handle non-finite values.
Results may differ from a plain program's by a relative error of at most 0.007.
The roundings to bfloat16 on the way count: a program that leaves them out, or rounds other values in their place, can miss the bound.
Values may be sent and summed in bfloat16 or wider, within the bound.
A program may use at most 64 MiB of HBM per device.

v0:
```python
import functools
import math

import jax
import jax.numpy as jnp
from jax import lax
from jax.experimental import pallas as pl
from jax.experimental.pallas import tpu as pltpu
from jax.sharding import PartitionSpec as P

step_size = 1.0


HEAD = 16


def slots_of(tokens, top, experts):
    cap = 5 * tokens * top // (4 * experts) + 1
    return (cap // 8 * 8, 1) if cap % 8 == 1 else (-(-cap // 8) * 8, 0)


def steps_kernel(
    count, experts, cuts, slots, over,
    pw_hbm, z_hbm, x_hbm, g_hbm, routing_hbm, gates_hbm, out_ref,
    pw, routing, gates, xb, gb, xs, ext, ext_in, ext_n, xin, xn, xt, xnt, zc, par, hid, rs, rr, second, came, sent, got,
    load_sem, cut_sem, ext_send, ext_recv, ext_fwd, tok_send, tok_recv, fwd_send, fwd_recv, r_send, r_recv,
    pair_send, pair_recv, line_send, line_recv, turn,
):
    bf16, f32 = jnp.bfloat16, jnp.float32
    node, mine = lax.axis_index("node"), lax.axis_index("expert")
    chips = count // 2
    chip, core = node // 2, node % 2
    low = (chip * 2 < chips).astype(jnp.int32)
    inner = (chip > 0) & (chip < chips - 1)
    other = chip * 2 + (1 - core)
    before = (node + count - 1) % count
    depth, width = zc.shape[1:]
    part = width // 3
    hidden = part * cuts
    rows = depth // count
    own = x_hbm.shape[0]
    total = HEAD + experts * slots
    padded = xin.shape[0]
    folds = 2 * depth // 128
    model_scale = 1.0 / math.sqrt(depth)
    hidden_scale = 1.0 / math.sqrt(hidden)
    tile_d = math.gcd(depth, 256)
    MESH = pl.DeviceIdType.MESH

    loads = [
        pltpu.make_async_copy(x_hbm, xb, load_sem.at[0]),
        pltpu.make_async_copy(g_hbm, gb, load_sem.at[1]),
    ]
    small_loads = [
        pltpu.make_async_copy(routing_hbm, routing, load_sem.at[2]),
        pltpu.make_async_copy(gates_hbm, gates, load_sem.at[3]),
        pltpu.make_async_copy(pw_hbm, pw, load_sem.at[4]),
    ]
    for copy in small_loads:
        copy.start()
    for copy in loads:
        copy.start()

    def cut_load(k, j):
        return pltpu.make_async_copy(
            z_hbm.at[:, pl.ds(j * hidden + k * part, part)],
            zc.at[k, :, pl.ds(j * part, part)],
            cut_sem.at[k, j],
        )

    barrier = pltpu.get_barrier_semaphore()
    for d in range(1, experts):
        pl.semaphore_signal(
            barrier, inc=1, device_id={"expert": mine ^ d}, device_id_type=MESH
        )
    for by in (1, count - 1, 2, count - 2):
        pl.semaphore_signal(
            barrier, inc=1, device_id={"node": (node + by) % count}, device_id_type=MESH
        )

    for copy in small_loads:
        copy.wait()

    def weight_at(by):
        return pw[(node + by + count) % count]

    def last_at(by):
        total_w = weight_at(by) + weight_at(by - 1) + weight_at(by - 2) + weight_at(by - 3)
        return jnp.full((1, width), total_w * 0.25, f32)

    def factor_at(by):
        return (0.5 / last_at(by) + 0.5 / last_at(by + 2)) / count

    factor = factor_at(1)
    keep = 0.5 * (factor_at(0) + factor)
    later = 1.0 / jnp.full((1, width), weight_at(1) + weight_at(0), f32)

    names = lax.broadcasted_iota(jnp.int32, (16, own), 0)
    first, second_of = routing[0:1, :] == names, routing[1:2, :] == names
    chosen_t = jnp.where(first, 1.0, jnp.where(second_of, 1.0, 0.0))
    weighed_t = jnp.where(first, gates[0:1, :], jnp.where(second_of, gates[1:2, :], 0.0))
    ahead = jnp.where(
        lax.broadcasted_iota(jnp.int32, (own, own), 0)
        < lax.broadcasted_iota(jnp.int32, (own, own), 1),
        1.0, 0.0,
    ).astype(bf16)
    place = jnp.dot(chosen_t.astype(bf16), ahead, preferred_element_type=f32)
    place = jnp.where(chosen_t > 0.0, place, -1.0)
    slot = lax.broadcasted_iota(jnp.int32, (slots, own), 0).astype(f32)
    picks = [jnp.where(place == float(slots), 1.0, 0.0)] + [jnp.where(slot == place[e : e + 1, :], 1.0, 0.0) for e in range(experts)]
    pick = jnp.concatenate(picks, axis=0).astype(bf16)
    weighings = [weighed_t] + [weighed_t[e : e + 1, :] for e in range(experts)]
    row_gates = jnp.concatenate(
        [jnp.sum(p * v, axis=1, keepdims=True) for p, v in zip(picks, weighings)], axis=0
    )

    for copy in loads:
        copy.wait()
    for k in range(cuts):
        for j in range(3):
            cut_load(k, j).start()
    wide = math.gcd(depth, 256)
    for i in range(depth // wide):
        at = slice(i * wide, (i + 1) * wide)
        moved_x = jnp.dot(pick, xb[:, at], preferred_element_type=f32)
        moved_g = row_gates * jnp.dot(pick, gb[:, at], preferred_element_type=f32)
        for h, moved in enumerate((moved_x, moved_g)):
            start = h * depth + i * wide
            for e in range(experts):
                of = slice(HEAD + e * slots, HEAD + (e + 1) * slots)
                xs[e, :, start : start + wide] = moved[of].astype(bf16)
                for c in range(wide // 128 if over else 0):
                    row = start // 128 + c
                    ext[e, row : row + 1, :] = moved[e : e + 1, c * 128 : (c + 1) * 128]

    pl.semaphore_wait(barrier, experts - 1 + 4)

    def block(d):
        return pl.ds(d * slots + (HEAD if d > 0 else 0), slots)

    halves = [pl.ds(0, depth), pl.ds(depth, depth)]

    def give(d, h):
        return pltpu.make_async_remote_copy(
            src_ref=xs.at[mine ^ d, :, halves[h]], dst_ref=xin.at[block(d), halves[h]],
            send_sem=tok_send.at[d, h], recv_sem=tok_recv.at[d, h],
            device_id={"expert": mine ^ d}, device_id_type=MESH,
        )

    def onward(d, h):
        source = xs.at[mine, :, halves[h]] if d == 0 else xin.at[block(d), halves[h]]
        return pltpu.make_async_remote_copy(
            src_ref=source, dst_ref=xn.at[block(d), halves[h]],
            send_sem=fwd_send.at[d, h], recv_sem=fwd_recv.at[d, h],
            device_id={"node": before}, device_id_type=MESH,
        )

    def give_over(d):
        return pltpu.make_async_remote_copy(
            src_ref=ext.at[mine ^ d], dst_ref=ext_in.at[d],
            send_sem=ext_send.at[d], recv_sem=ext_recv.at[d],
            device_id={"expert": mine ^ d}, device_id_type=MESH,
        )

    def onward_over():
        return pltpu.make_async_remote_copy(
            src_ref=ext_in, dst_ref=ext_n, send_sem=ext_fwd.at[0], recv_sem=ext_fwd.at[1],
            device_id={"node": before}, device_id_type=MESH,
        )

    def unfold(source, target):
        lines = []
        for d in range(experts):
            value = source[d]
            lines.append(jnp.concatenate([value[c : c + 1] for c in range(folds)], axis=1))
        lines.append(jnp.zeros((HEAD - experts, 2 * depth), f32))
        target[slots : slots + HEAD, :] = jnp.concatenate(lines, axis=0).astype(bf16)

    def give_all():
        for d in range(1, experts if over else 0):
            give_over(d).start()
        for d in range(1, experts):
            for h in range(2):
                give(d, h).start()

    def arrive(d, h):
        give(d, h).wait_recv()
        onward(d, h).start()

    def result(k):
        return pltpu.make_async_remote_copy(
            src_ref=rs.at[k], dst_ref=rr.at[k],
            send_sem=r_send.at[k], recv_sem=r_recv.at[k],
            device_id={"node": before}, device_id_type=MESH,
        )

    def pair(k, t):
        return pltpu.make_async_remote_copy(
            src_ref=second.at[k, t, 1 - core], dst_ref=came.at[k, t],
            send_sem=pair_send.at[k, t], recv_sem=pair_recv.at[k, t],
            device_id={"node": other}, device_id_type=MESH,
        )

    def line(way, k, t):
        return pltpu.make_async_remote_copy(
            src_ref=sent.at[way, k, t], dst_ref=got.at[way, k, t],
            send_sem=line_send.at[way, k, t], recv_sem=line_recv.at[way, k, t],
            device_id={"node": (node + (2 if way == 0 else count - 2)) % count},
            device_id_type=MESH,
        )

    @pl.when(core == 0)
    def _():
        give_all()

    for h in range(2):
        onward(0, h).start()
    xin[:slots, :] = xs[mine]
    if over:
        ext_in[0] = ext[mine]
    else:
        xin[slots : slots + HEAD, :] = jnp.zeros((HEAD, 2 * depth), bf16)
        xn[slots : slots + HEAD, :] = jnp.zeros((HEAD, 2 * depth), bf16)
    if padded > total:
        xin[total:, :] = jnp.zeros((padded - total, 2 * depth), bf16)
        xn[total:, :] = jnp.zeros((padded - total, 2 * depth), bf16)
        for k in range(cuts):
            hid[k, total:, :] = jnp.zeros((padded - total, width), bf16)

    weight = weight_at(0)
    for k in range(cuts):
        for j in range(3):
            cut_load(k, j).wait()

    @pl.loop(0, cuts)
    def _(k):
        @pl.loop(0, depth // tile_d)
        def _(i):
            at = pl.ds(pl.multiple_of(i * tile_d, tile_d), tile_d)
            par[k, at, :] = (zc[k, at, :].astype(f32) / weight).astype(bf16)

    def turned(source, target, tile, part_of=(0, 2)):
        at = slice(tile * 128, (tile + 1) * 128)
        step = math.gcd(depth, 512)

        @pl.loop(part_of[0] * (depth // step), part_of[1] * (depth // step))
        def _(i):
            cols = pl.ds(pl.multiple_of(i * step, step), step)
            target[cols, at] = source[at, cols].T

    def next_head():
        if over:
            onward_over().wait_recv()
            unfold(ext_n, xn)

    def activations(pre, act, scale, hid_scale):
        gate = pre[:, :part] * scale
        upper = pre[:, part:] * scale
        act = act * hid_scale
        sig = jax.nn.sigmoid(gate)
        return (
            (act * upper * sig * (1.0 + gate * (1.0 - sig))).astype(bf16),
            (act * gate * sig).astype(bf16),
            (gate * sig * upper).astype(bf16),
        )

    def put(k, at, parts):
        for j in range(3):
            hid[k, at, j * part : (j + 1) * part] = parts[j]

    def forward_cut(k, at):
        pre = jnp.dot(xin[at, :depth], par[k, :, : 2 * part], preferred_element_type=f32)
        act = jnp.dot(xin[at, depth:], par[k, :, 2 * part :], preferred_element_type=f32)
        put(k, at, activations(pre, act, model_scale, hidden_scale))

    def forward(at):
        @pl.loop(0, cuts)
        def _(k):
            forward_cut(k, at)

    def gradients(xt, k, at, size):
        down_at = pl.ds(pl.multiple_of(at + depth, size), size)
        at = pl.ds(pl.multiple_of(at, size), size)
        both = jnp.dot(xt[at, :], hid[k, :, : 2 * part], preferred_element_type=f32)
        down = jnp.dot(xt[down_at, :], hid[k, :, 2 * part :], preferred_element_type=f32)
        return jnp.concatenate([both * model_scale, down * hidden_scale], axis=1)

    forward(slice(0, slots))

    @pl.when(core == 1)
    def _():
        pl.semaphore_wait(turn, 1)
        give_all()

    tiles = padded // 128
    last = experts - 1
    final = HEAD + last * slots
    early = final // 128

    if over:
        for d in range(1, experts):
            give_over(d).wait_recv()
        onward_over().start()
        unfold(ext_in, xin)

    for h in range(2):
        for d in range(1, last):
            arrive(d, h)
    for tile in range(early):
        turned(xin, xt, tile)
    forward(slice(slots, final))

    def next_tiles():
        next_head()
        for h in range(2):
            for d in range(last):
                onward(d, h).wait_recv()
        for tile in range(early):
            turned(xn, xnt, tile)
        for h in range(2):
            onward(last, h).wait_recv()
        for tile in range(early, tiles):
            turned(xn, xnt, tile)

    arrive(last, 0)
    for tile in range(early, tiles):
        turned(xin, xt, tile, (0, 1))

    @pl.when(core == 0)
    def _():
        for d in range(1, experts):
            for h in range(1 if d == last else 2):
                give(d, h).wait_send()
        pl.semaphore_signal(turn, inc=1, device_id={"node": other}, device_id_type=MESH)

    pl.when(core == 1)(next_tiles)

    arrive(last, 1)
    for tile in range(early, tiles):
        turned(xin, xt, tile, (1, 2))

    def round_one(k):
        forward_cut(k, slice(final, total))

        @pl.loop(0, depth // tile_d)
        def _(i):
            at = pl.ds(pl.multiple_of(i * tile_d, tile_d), tile_d)
            grads = gradients(xt, k, i * tile_d, tile_d)
            zc[k, at, :] = (zc[k, at, :].astype(f32) - step_size * grads).astype(bf16)

        pre = jnp.dot(xin[:total, :depth], zc[k, :, : 2 * part], preferred_element_type=f32)
        act = jnp.dot(xin[:total, depth:], zc[k, :, 2 * part :], preferred_element_type=f32)
        rs[k, :, : 2 * part] = pre.astype(bf16)
        rs[k, :, 2 * part :] = act.astype(bf16)
        result(k).start()

    def round_two(k):
        pre = jnp.dot(xn[:total, :depth], zc[k, :, : 2 * part], preferred_element_type=f32)
        act = jnp.dot(xn[:total, depth:], zc[k, :, 2 * part :], preferred_element_type=f32)
        result(k).wait_recv()
        pre = pre + rr[k, :, : 2 * part].astype(f32)
        act = act + rr[k, :, 2 * part :].astype(f32)
        parts = activations(
            pre, act, later[:, :1] * model_scale, later[:, :1] * hidden_scale
        )
        put(k, slice(0, total), parts)

        @pl.loop(0, chips)
        def _(i):
            t = i + low * (chips - 1 - 2 * i)
            at = pl.ds(pl.multiple_of(t * 2 * rows, 2 * rows), 2 * rows)
            grads = gradients(xnt, k, t * 2 * rows, 2 * rows)
            value = (keep * zc[k, at, :].astype(f32) - (step_size * factor) * grads).astype(bf16)
            second[k, t, 0] = value[:rows]
            second[k, t, 1] = value[rows:]
            pair(k, t).start()

    def term(k, t):
        return second[k, t, core].astype(f32) + came[k, t].astype(f32)

    def rising(k, j):
        t = chips - 1 - j
        pair(k, t).wait_recv()
        sent[0, k, t] = term(k, t).astype(bf16)

        @pl.when(chip > 0)
        def _():
            line(0, k, t).wait_recv()
            sent[0, k, t] = (term(k, t) + got[0, k, t].astype(f32)).astype(bf16)

        line(0, k, t).start()

    def falling(k, t):
        pair(k, t).wait_recv()
        sent[1, k, t] = term(k, t).astype(bf16)

        @pl.when(chip < chips - 1)
        def _():
            line(1, k, t).wait_recv()
            sent[1, k, t] = (term(k, t) + got[1, k, t].astype(f32)).astype(bf16)

        line(1, k, t).start()

    def send_sums(k):
        up = chips - 1 - chip - (chip == 0).astype(jnp.int32)
        down = chip - (chip == chips - 1).astype(jnp.int32)

        def rise(j, carry):
            rising(k, j)
            return carry

        def fall(t, carry):
            falling(k, t)
            return carry

        @pl.when(chip * 2 < chips)
        def _():
            lax.fori_loop(0, up, rise, 0)
            lax.fori_loop(0, down, fall, 0)

        @pl.when(chip * 2 >= chips)
        def _():
            lax.fori_loop(0, down, fall, 0)
            lax.fori_loop(0, up, rise, 0)

    def finish(k):
        pair(k, chip).wait_recv()
        value = term(k, chip)
        for j in range(3):
            out_ref[:, j * hidden + k * part : j * hidden + (k + 1) * part] = value[
                :, j * part : (j + 1) * part
            ]
        for way, there in ((0, chip > 0), (1, chip < chips - 1)):

            @pl.when(there)
            def _():
                line(way, k, chip).wait_recv()
                for j in range(3):
                    at = slice(j * hidden + k * part, j * hidden + (k + 1) * part)
                    cols = slice(j * part, (j + 1) * part)
                    out_ref[:, at] = out_ref[:, at] + got[way, k, chip, :, cols].astype(f32)

    @pl.when(core == 0)
    def _():
        pl.loop(0, cuts)(round_one)
        next_tiles()

    @pl.when(core == 1)
    def _():
        round_one(0)

    @pl.loop(0, cuts)
    def _(k):
        round_two(k)

        @pl.when(inner & (k > 0))
        def _():
            send_sums(k - 1)

        @pl.when(jnp.logical_not(inner))
        def _():
            send_sums(k)

        @pl.when((core == 1) & (k < cuts - 1))
        def _():
            round_one(k + 1)

    @pl.when(inner)
    def _():
        send_sums(cuts - 1)

    def nearest(k, carry):
        @pl.when(chip == 0)
        def _():
            rising(k, chips - 2)

        @pl.when(chip == chips - 1)
        def _():
            falling(k, chips - 2)

        return carry

    lax.fori_loop(0, cuts, nearest, 0)

    for k in range(cuts):
        finish(k)

    @pl.when(core == 1)
    def _():
        for d in range(1, experts):
            for h in range(2):
                give(d, h).wait_send()

    @pl.when(core == 0)
    def _():
        give(last, 1).wait_send()

    if over:
        onward_over().wait_send()
        for d in range(1, experts):
            give_over(d).wait_send()

    for d in range(experts):
        for h in range(2):
            onward(d, h).wait_send()

    def drain(k, carry):
        result(k).wait_send()

        def both(t, c):
            pair(k, t).wait_send()
            return c

        lax.fori_loop(0, chips, both, 0)

        def up(t, c):
            line(0, k, t).wait_send()
            return c

        def down(t, c):
            line(1, k, t).wait_send()
            return c

        lax.fori_loop(chip + 1, chips, up, 0)
        lax.fori_loop(0, chip, down, 0)
        return carry

    lax.fori_loop(0, cuts, drain, 0)


def local(numerators, push_weights, tokens, cotangent, routing, gates):
    bf16, f32 = jnp.bfloat16, jnp.float32
    count, experts = lax.axis_size("node"), lax.axis_size("expert")
    depth, columns = numerators.shape[2:]
    own, top = routing.shape[1:]
    hidden = columns // 3
    part = math.gcd(hidden, 128)
    cuts = hidden // part
    width = 3 * part
    chips, rows = count // 2, depth // count
    slots, over = slots_of(own, top, experts)
    total = HEAD + experts * slots
    folds = 2 * depth // 128
    padded = -(-total // 128) * 128
    vmem = pl.BlockSpec(memory_space=pltpu.VMEM)
    anywhere = pl.BlockSpec(memory_space=pltpu.HBM)
    dma = pltpu.SemaphoreType.DMA
    operands = [
        pltpu.with_memory_space_constraint(value, pltpu.HBM)
        for value in (
            push_weights, numerators[0, 0], tokens[0], cotangent[0], routing[0].T, gates[0].T
        )
    ]
    out = pl.pallas_call(
        functools.partial(steps_kernel, count, experts, cuts, slots, over),
        out_shape=jax.ShapeDtypeStruct((rows, columns), f32),
        in_specs=[anywhere] * 6,
        out_specs=vmem,
        scratch_shapes=[
            pltpu.SMEM((count,), f32),
            pltpu.VMEM((top, own), jnp.int32),
            pltpu.VMEM((top, own), f32),
            pltpu.VMEM((own, depth), bf16),
            pltpu.VMEM((own, depth), bf16),
            pltpu.VMEM((experts, slots, 2 * depth), bf16),
            pltpu.VMEM((experts, folds, 128), f32),
            pltpu.VMEM((experts, folds, 128), f32),
            pltpu.VMEM((experts, folds, 128), f32),
            pltpu.VMEM((padded, 2 * depth), bf16),
            pltpu.VMEM((padded, 2 * depth), bf16),
            pltpu.VMEM((2 * depth, padded), bf16),
            pltpu.VMEM((2 * depth, padded), bf16),
            pltpu.VMEM((cuts, depth, width), bf16),
            pltpu.VMEM((cuts, depth, width), bf16),
            pltpu.VMEM((cuts, padded, width), bf16),
            pltpu.VMEM((cuts, total, width), bf16),
            pltpu.VMEM((cuts, total, width), bf16),
            pltpu.VMEM((cuts, chips, 2, rows, width), bf16),
            pltpu.VMEM((cuts, chips, rows, width), bf16),
            pltpu.VMEM((2, cuts, chips, rows, width), bf16),
            pltpu.VMEM((2, cuts, chips, rows, width), bf16),
            dma((5,)),
            dma((cuts, 3)),
            dma((experts,)),
            dma((experts,)),
            dma((2,)),
            dma((experts, 2)),
            dma((experts, 2)),
            dma((experts, 2)),
            dma((experts, 2)),
            dma((cuts,)),
            dma((cuts,)),
            dma((cuts, chips)),
            dma((cuts, chips)),
            dma((2, cuts, chips)),
            dma((2, cuts, chips)),
            pltpu.SemaphoreType.REGULAR,
        ],
        compiler_params=pltpu.CompilerParams(
            collective_id=0, has_side_effects=True, vmem_limit_bytes=52 * 1024 * 1024
        ),
    )(*operands)
    return out[None]


def solution(mesh):
    placed = (
        P("node", "expert", None, None),
        P(),
        P("node", "expert", None),
        P("node", "expert", None),
        P("node", "expert", None),
        P("node", "expert", None),
    )
    return jax.shard_map(
        local, mesh=mesh, in_specs=placed, out_specs=P("expert", "node", None), check_vma=False
    )
```

profile of v0, /device:TPU:0, one launch (start us, length us, event | category | flops | bytes accessed | tf_op | source)
XLA Modules:
  0.0 79.8 jit_solution(12212255544958234959)
XLA Ops:
  0.0 78.8 %shard_map.64 = f32[192,1536]{1,0:T(8,128)S(1)} custom-call(f32[8]{0:T(128)} %pw_hbm.1, bf16[1536,1536]{1,0:T(8,128)(2,1)} %bitcast.11, bf16[128,1536]{1,0:T(8,128)(2,1)} %bitcast.12, bf16[128,1536]{1,0:T(8,128)(2,1)} %bitcast.13, s32[2,128]{1,0:T(2,128)} %bitcast.14, f32[2,128]{1,0:T(2,128)} %bitcast.15), custom_call_target="tpu_custom_call" | custom-call | tf_op jit(solution)/shard_map/pallas_call | solution.py:554
  78.8 1.0 %copy.8 = f32[1,192,1536]{2,1,0:T(8,128)} copy(f32[1,192,1536]{2,1,0:T(8,128)S(1)} %bitcast.10) | data formatting | bytes 2359296
where the time goes:
time: 80 us; the launch traced here: 79.8 us
  Pallas kernels  78.8 us (98%)
  local copies, waits for them, and re-layouts  1.02 us (1%)
    pallas_call x1, Pallas kernels, local(): pl.pallas_call(functools.partial(steps_kernel, count, experts, cuts, slot...  78.8 us

commit v1 on v0

--- a/solution.py
+++ b/solution.py
@@ -22,7 +22,7 @@
 def steps_kernel(
     count, experts, cuts, slots, over,
     pw_hbm, z_hbm, x_hbm, g_hbm, routing_hbm, gates_hbm, out_ref,
-    pw, routing, gates, xb, gb, xs, ext, ext_in, ext_n, xin, xn, xt, xnt, zc, par, hid, rs, rr, second, came, sent, got,
+    pw, routing, gates, xb, gb, xs, lines, ext, ext_in, ext_n, xin, xn, xt, xnt, zc, par, hid, rs, rr, second, came, sent, got,
     load_sem, cut_sem, ext_send, ext_recv, ext_fwd, tok_send, tok_recv, fwd_send, fwd_recv, r_send, r_recv,
     pair_send, pair_recv, line_send, line_recv, turn,
 ):
@@ -131,7 +131,9 @@
                 xs[e, :, start : start + wide] = moved[of].astype(bf16)
                 for c in range(wide // 128 if over else 0):
                     row = start // 128 + c
-                    ext[e, row : row + 1, :] = moved[e : e + 1, c * 128 : (c + 1) * 128]
+                    lines[e, row : row + 1, :] = moved[e : e + 1, c * 128 : (c + 1) * 128]
+    if over:
+        ext[...] = lines[...].astype(bf16)
 
     pl.semaphore_wait(barrier, experts - 1 + 4)
 
@@ -169,12 +171,12 @@
         )
 
     def unfold(source, target):
-        lines = []
+        whole = []
         for d in range(experts):
-            value = source[d]
-            lines.append(jnp.concatenate([value[c : c + 1] for c in range(folds)], axis=1))
-        lines.append(jnp.zeros((HEAD - experts, 2 * depth), f32))
-        target[slots : slots + HEAD, :] = jnp.concatenate(lines, axis=0).astype(bf16)
+            value = source[d].astype(f32)
+            whole.append(jnp.concatenate([value[c : c + 1] for c in range(folds)], axis=1))
+        whole.append(jnp.zeros((HEAD - experts, 2 * depth), f32))
+        target[slots : slots + HEAD, :] = jnp.concatenate(whole, axis=0).astype(bf16)
 
     def give_all():
         for d in range(1, experts if over else 0):
@@ -342,11 +344,8 @@
     def round_one(k):
         forward_cut(k, slice(final, total))
 
-        @pl.loop(0, depth // tile_d)
-        def _(i):
-            at = pl.ds(pl.multiple_of(i * tile_d, tile_d), tile_d)
-            grads = gradients(xt, k, i * tile_d, tile_d)
-            zc[k, at, :] = (zc[k, at, :].astype(f32) - step_size * grads).astype(bf16)
+        grads = gradients(xt, k, 0, depth)
+        zc[k] = (zc[k].astype(f32) - step_size * grads).astype(bf16)
 
         pre = jnp.dot(xin[:total, :depth], zc[k, :, : 2 * part], preferred_element_type=f32)
         act = jnp.dot(xin[:total, depth:], zc[k, :, 2 * part :], preferred_element_type=f32)
@@ -365,7 +364,7 @@
         )
         put(k, slice(0, total), parts)
 
-        @pl.loop(0, chips)
+        @pl.loop(0, chips, unroll=2)
         def _(i):
             t = i + low * (chips - 1 - 2 * i)
             at = pl.ds(pl.multiple_of(t * 2 * rows, 2 * rows), 2 * rows)
@@ -401,27 +400,27 @@
 
         line(1, k, t).start()
 
-    def send_sums(k):
-        up = chips - 1 - chip - (chip == 0).astype(jnp.int32)
-        down = chip - (chip == chips - 1).astype(jnp.int32)
-
+    def rise_all(k):
         def rise(j, carry):
             rising(k, j)
             return carry
 
+        lax.fori_loop(0, chips - 1 - chip - (chip == 0).astype(jnp.int32), rise, 0)
+
+    def fall_all(k):
         def fall(t, carry):
             falling(k, t)
             return carry
 
-        @pl.when(chip * 2 < chips)
-        def _():
-            lax.fori_loop(0, up, rise, 0)
-            lax.fori_loop(0, down, fall, 0)
-
-        @pl.when(chip * 2 >= chips)
-        def _():
-            lax.fori_loop(0, down, fall, 0)
-            lax.fori_loop(0, up, rise, 0)
+        lax.fori_loop(0, chip - (chip == chips - 1).astype(jnp.int32), fall, 0)
+
+    def long_way(k):
+        pl.when(low == 1)(functools.partial(rise_all, k))
+        pl.when(low == 0)(functools.partial(fall_all, k))
+
+    def short_way(k):
+        pl.when(low == 1)(functools.partial(fall_all, k))
+        pl.when(low == 0)(functools.partial(rise_all, k))
 
     def finish(k):
         pair(k, chip).wait_recv()
@@ -453,21 +452,27 @@
     def _(k):
         round_two(k)
 
-        @pl.when(inner & (k > 0))
+        ready = k - inner.astype(jnp.int32)
+
+        @pl.when(ready >= 0)
         def _():
-            send_sums(k - 1)
-
-        @pl.when(jnp.logical_not(inner))
-        def _():
-            send_sums(k)
+            long_way(ready)
 
         @pl.when((core == 1) & (k < cuts - 1))
         def _():
             round_one(k + 1)
 
+        behind = k - 2 * inner.astype(jnp.int32)
+
+        @pl.when(behind >= 0)
+        def _():
+            short_way(behind)
+
     @pl.when(inner)
     def _():
-        send_sums(cuts - 1)
+        long_way(cuts - 1)
+        for k in range(max(cuts - 2, 0), cuts):
+            short_way(k)
 
     def nearest(k, carry):
         @pl.when(chip == 0)
@@ -564,8 +569,9 @@
             pltpu.VMEM((own, depth), bf16),
             pltpu.VMEM((experts, slots, 2 * depth), bf16),
             pltpu.VMEM((experts, folds, 128), f32),
-            pltpu.VMEM((experts, folds, 128), f32),
-            pltpu.VMEM((experts, folds, 128), f32),
+            pltpu.VMEM((experts, folds, 128), bf16),
+            pltpu.VMEM((experts, folds, 128), bf16),
+            pltpu.VMEM((experts, folds, 128), bf16),
             pltpu.VMEM((padded, 2 * depth), bf16),
             pltpu.VMEM((padded, 2 * depth), bf16),
             pltpu.VMEM((2 * depth, padded), bf16),

time: 80 us -> 79.4 us (level)
  no operation moved by 1% of the time
where the time goes in v1:
time: 79.4 us; the launch traced here: 79.2 us
  Pallas kernels  78.2 us (98%)
  local copies, waits for them, and re-layouts  1.02 us (1%)
    pallas_call x1, Pallas kernels, local(): pl.pallas_call(functools.partial(steps_kernel, count, experts, cuts, slot...  78.2 us

profile of v1, /device:TPU:0, one launch (start us, length us, event | category | flops | bytes accessed | tf_op | source)
XLA Modules:
  0.0 79.2 jit_solution(2168262394863132491)
XLA Ops:
  0.0 78.2 %shard_map.64 = f32[192,1536]{1,0:T(8,128)S(1)} custom-call(f32[8]{0:T(128)} %pw_hbm.1, bf16[1536,1536]{1,0:T(8,128)(2,1)} %bitcast.11, bf16[128,1536]{1,0:T(8,128)(2,1)} %bitcast.12, bf16[128,1536]{1,0:T(8,128)(2,1)} %bitcast.13, s32[2,128]{1,0:T(2,128)} %bitcast.14, f32[2,128]{1,0:T(2,128)} %bitcast.15), custom_call_target="tpu_custom_call" | custom-call | tf_op jit(solution)/shard_map/pallas_call | solution.py:559
  78.2 1.0 %copy.8 = f32[1,192,1536]{2,1,0:T(8,128)} copy(f32[1,192,1536]{2,1,0:T(8,128)S(1)} %bitcast.10) | data formatting | bytes 2359296
